TPU v7x, 32 devices: a whole 2x2x4 slice. The times are simulated.
32 devices in a mesh: band: 16 (over z, y, core), fft: 2 (over x).
Axes of the slice: x: 2, y: 2, z: 4, core: 2. Of those that a mesh axis runs over, the one named last changes fastest.
Arguments:
- coefficients: float32 [16, 2, 72, 5184], P('band', None, None, 'fft'), may hold values from -0.009765625 to 0.009765625
- col_index: int32 [5184], replicated, may hold values from 0 to 5183, each once
- occupation: int32 [16], P('band'), may hold values from 1 to 4
Outputs:
- density: float32 [288, 288, 288], P('band', 'fft')
Inputs may be any that keep to these rules, and one draw needn't show every extreme that they name: `col_index`: each number of the range appears once.
All inputs are finite; a program needn't handle non-finite values.
Results may differ from a plain program's by a relative error of at most 0.0003.
Values sent between devices are 32-bit elements; how exact they have to be, the bound alone decides.
A program may use at most 128 MiB of HBM per device.

v0:
```python
import math

import jax
import jax.numpy as jnp
from jax import lax
from jax.sharding import PartitionSpec as P

NC = 144
NF = 288
KZ = 72
NCOLS = 5184


def product(pattern, operand_a, operand_b):
    return jnp.einsum(pattern, operand_a, operand_b, precision=lax.Precision.HIGHEST)


def phase_tables(wave_count, offset, points):
    wave_index = jnp.arange(wave_count, dtype=jnp.int32) - offset
    grid_index = jnp.arange(points, dtype=jnp.int32)
    phases = jnp.mod(wave_index[:, None] * grid_index[None, :], points)
    angles = phases.astype(jnp.float32) * (2.0 * math.pi / points)
    return (jnp.cos(angles), jnp.sin(angles))


def interpolation_matrix(coarse_len, fine_len):
    fine_index = jnp.arange(fine_len, dtype=jnp.int32)
    coarse_index = jnp.arange(coarse_len, dtype=jnp.int32)
    wave_index = jnp.arange(1, coarse_len // 2, dtype=jnp.int32)
    offsets = fine_index[:, None] - 2 * coarse_index[None, :]
    phases = jnp.mod(offsets[:, :, None] * wave_index[None, None, :], fine_len)
    angles = phases.astype(jnp.float32) * (2.0 * math.pi / fine_len)
    return (1.0 + 2.0 * jnp.sum(jnp.cos(angles), axis=2)) / coarse_len


def rotate(pattern, real_part, imag_part, cos_table, sin_table):
    out_real = product(pattern, real_part, cos_table) - product(pattern, imag_part, sin_table)
    out_imag = product(pattern, real_part, sin_table) + product(pattern, imag_part, cos_table)
    return (out_real, out_imag)


def local(coefficients, col_index, occupation):
    band_here = coefficients.shape[0]
    col_count = coefficients.shape[3]
    band_total = band_here * lax.axis_size("band")
    radius = KZ // 2
    col_start = lax.axis_index("fft") * col_count
    local_cols = lax.dynamic_slice_in_dim(col_index, col_start, col_count)
    first_wave = local_cols // KZ - radius
    second_wave = local_cols % KZ - radius
    third_wave = jnp.arange(KZ, dtype=jnp.int32) - radius
    radial = (first_wave * first_wave + second_wave * second_wave)[None, :] + (
        third_wave * third_wave
    )[:, None]
    inside = (radial <= radius * radius).astype(jnp.float32)
    masked = coefficients * inside
    cos_table, sin_table = phase_tables(KZ, radius, NC)
    line_real, line_imag = rotate("bkc,kz->bzc", masked[:, 0], masked[:, 1], cos_table, sin_table)
    z_lines = jnp.stack([line_real, line_imag], axis=1)
    inverse = jnp.zeros((NCOLS,), jnp.int32).at[col_index].set(jnp.arange(NCOLS, dtype=jnp.int32))
    block_in = lax.all_to_all(z_lines, "fft", split_axis=2, concat_axis=3, tiled=True)
    box_grid = jnp.take(block_in, inverse, axis=3)
    box_grid = box_grid.reshape(block_in.shape[0], 2, block_in.shape[2], KZ, KZ)
    half_real, half_imag = rotate(
        "bzak,kr->bzar", box_grid[:, 0], box_grid[:, 1], cos_table, sin_table
    )
    full_real, full_imag = rotate("bzar,as->bzsr", half_real, half_imag, cos_table, sin_table)
    moduli = full_real * full_real + full_imag * full_imag
    weights = occupation.astype(jnp.float32) / band_total
    partial_value = product("b,bzxy->zxy", weights, moduli)
    interpolation = interpolation_matrix(NC, NF)
    row_share = NF // lax.axis_size("band")
    summed = lax.psum(partial_value, "band")
    own_rows = lax.dynamic_slice_in_dim(
        interpolation, lax.axis_index("band") * row_share, row_share, 0
    )
    reduced = product("zgb,fb->zgf", product("zab,ga->zgb", summed, own_rows), interpolation)
    return product(
        "rgf,hr->gfh",
        lax.all_to_all(reduced, "fft", split_axis=2, concat_axis=0, tiled=True),
        interpolation,
    )


def solution(mesh):
    return jax.shard_map(
        local,
        mesh=mesh,
        in_specs=(P("band", None, None, "fft"), P(), P("band")),
        out_specs=P("band", "fft", None),
        check_vma=False,
    )
```

profile of v0, /device:TPU:0, one launch (start us, length us, event | category | flops | bytes accessed | tf_op | source)
XLA Modules:
  0.0 451.8 jit_solution(9786847167849780601)
XLA Ops:
  7.5 1.6 broadcast_multiply_fusion
  9.1 1.6 fusion.18
  10.7 1.6 fusion.19
  12.4 1.7 fusion.8
  14.1 1.7 fusion.7
  16.0 3.2 copy.44
  19.3 4.2 all-to-all-start
  23.5 36.3 %scatter_custom_fusion = s32[5184]{0:T(1024)S(1)} fusion(s32[5184]{0:T(1024)S(1)} %compare_select_fusion.1, s32[5184]{0:T(1024)S(1)} %iota.59, s32[]{:T(128)} %constant.53.clone.1), kind=kCustom, calls=%fused_computation.112 | custom fusion | bytes 20740 | tf_op jit(solution)/shard_map/scatter | solution.py:60
  60.6 6.9 %copy.62 = f32[1,2,72,2,2592]{2,1,4,3,0:T(2,128)} copy(f32[1,2,72,2,2592]{4,1,2,3,0:T(2,128)S(1)} %bitcast.89) | data formatting | bytes 5971968 | tf_op jit(solution)/shard_map/all_to_all | solution.py:61
  67.5 19.1 %gather_fusion = f32[5184,2,72]{2,1,0:T(2,128)} fusion(f32[2,72,5184]{1,0,2:T(2,128)} %bitcast.87, s32[6144]{0:T(1024)S(1)} %pad_clamp_fusion), kind=kCustom, calls=%fused_computation | custom fusion | bytes 5992704 | tf_op jit(solution)/shard_map/jit(_take)/gather | solution.py:62
  86.6 8.5 %copy.63 = f32[1,2,72,72,72]{4,3,2,1,0:T(8,128)} copy(f32[1,2,72,72,72]{2,1,4,3,0:T(2,128)} %bitcast.88) | data formatting | bytes 5971968 | tf_op jit(solution)/shard_map/jit(_take)/gather | solution.py:62
  95.0 2.9 broadcast_select_fusion
  97.9 4.8 %fusion.10 = f32[72,72,144]{2,1,0:T(8,128)S(1)} fusion(f32[1,2,72,72,72]{4,3,2,1,0:T(8,128)S(1)} %broadcast_select_fusion, s32[72]{0:T(128)S(1)} %iota_add_fusion), kind=kOutput, calls=%fused_computation.22 | convolution fusion | flops 645065856 | bytes 5640704 | tf_op jit(solution)/shard_map/bzak,kr->bzar/dot_general | solution.py:15
  102.7 4.8 %fusion.13 = f32[72,72,144]{2,1,0:T(8,128)S(1)} fusion(f32[72,72,144]{2,1,0:T(8,128)S(1)} %fusion.10, f32[1,2,72,72,72]{4,3,2,1,0:T(8,128)S(1)} %broadcast_select_fusion, s32[72]{0:T(128)S(1)} %iota_add_fusion), kind=kOutput, calls=%fused_computation.25 | convolution fusion | flops 645812352 | bytes 10949120 | tf_op jit(solution)/shard_map/bzak,kr->bzar/dot_general | solution.py:15
  107.5 11.8 %fusion.26 = f32[144,72,144]{2,0,1:T(8,128)} fusion(f32[72,72,144]{2,1,0:T(8,128)S(1)} %fusion.13, s32[72]{0:T(128)S(1)} %iota_add_fusion), kind=kOutput, calls=%fused_computation.46 | convolution fusion | flops 1290038400 | bytes 8958240 | tf_op jit(solution)/shard_map/bzar,as->bzsr/dot_general | solution.py:15
  119.3 12.0 %fusion.34 = f32[144,72,144]{2,0,1:T(8,128)} fusion(f32[72,72,144]{2,1,0:T(8,128)S(1)} %fusion.13, s32[72]{0:T(128)S(1)} %iota_add_fusion), kind=kOutput, calls=%fused_computation.54 | convolution fusion | flops 1290038400 | bytes 8958240 | tf_op jit(solution)/shard_map/bzar,as->bzsr/dot_general | solution.py:15
  131.3 4.8 %fusion.9 = f32[72,72,144]{2,1,0:T(8,128)S(1)} fusion(f32[1,2,72,72,72]{4,3,2,1,0:T(8,128)S(1)} %broadcast_select_fusion, s32[72]{0:T(128)S(1)} %iota_add_fusion), kind=kOutput, calls=%fused_computation.21 | convolution fusion | flops 645065856 | bytes 5640704 | tf_op jit(solution)/shard_map/bzak,kr->bzar/dot_general | solution.py:15
  136.1 4.8 %fusion.14 = f32[72,72,144]{2,1,0:T(8,128)S(1)} fusion(f32[72,72,144]{2,1,0:T(8,128)S(1)} %fusion.9, f32[1,2,72,72,72]{4,3,2,1,0:T(8,128)S(1)} %broadcast_select_fusion, s32[72]{0:T(128)S(1)} %iota_add_fusion), kind=kOutput, calls=%fused_computation.26 | convolution fusion | flops 645812352 | bytes 10949120 | tf_op jit(solution)/shard_map/bzak,kr->bzar/dot_general | solution.py:15
  140.9 11.7 %fusion.28 = f32[144,72,144]{2,0,1:T(8,128)} fusion(f32[72,72,144]{2,1,0:T(8,128)S(1)} %fusion.14, s32[72]{0:T(128)S(1)} %iota_add_fusion), kind=kOutput, calls=%fused_computation.48 | convolution fusion | flops 1290038400 | bytes 8958240 | tf_op jit(solution)/shard_map/bzar,as->bzsr/dot_general | solution.py:15
  152.6 21.9 %multiply_bitcast_fusion = f32[72,144,144]{2,1,0:T(8,128)} fusion(f32[144,72,144]{2,0,1:T(8,128)} %fusion.26, f32[144,72,144]{2,0,1:T(8,128)} %fusion.34, f32[144,72,144]{2,0,1:T(8,128)} %fusion.28, f32[]{:T(128)} %bitcast.1, f32[72,72,144]{2,1,0:T(8,128)} %copy-done, s32[72]{0:T(128)S(1)} %iota_add_fusion), kind=kOutput, calls=%fused_computation.11 | convolution fusion | flops 1298996352 | bytes 26874148 | tf_op jit(solution)/shard_map/bzar,as->bzsr/dot_general | solution.py:15
  174.6 61.2 %fusion.3 = f32[288,144]{0,1:T(8,128)S(1)} fusion(s32[71]{0:T(128)S(1)} %iota_add_fusion.1, s32[288,144]{0,1:T(8,128)S(1)} %iota_subtract_fusion), kind=kLoop, calls=%fused_computation.6 | loop fusion | flops 29403648 | bytes 332060 | tf_op jit(solution)/shard_map/reduce_sum | solution.py:33
  235.9 144.0 %all-reduce.2.cloned.1.call-done = f32[72,144,144]{2,1,0:T(8,128)} async-done(((f32[72,144,144]{2,1,0:T(8,128)}), f32[72,144,144]{2,1,0:T(8,128)}) %all-reduce.2.cloned.1.call-update) | async-done | bytes 5971984 | tf_op jit(solution)/shard_map/psum | solution.py:73
  379.9 8.3 %convolution_bitcast_fusion = f32[72,18,144]{2,1,0:T(8,128)S(1)} fusion(f32[72,144,144]{2,1,0:T(8,128)} %all-reduce.2.cloned.1.call-done, f32[288,144]{0,1:T(8,128)S(1)} %add_multiply_fusion, s32[]{:T(128)S(6)} %select_n.74), kind=kOutput, calls=%fused_computation.27 | convolution fusion | flops 322486272 | bytes 6792196 | tf_op jit(solution)/shard_map/zab,ga->zgb/dot_general | solution.py:15
  388.2 3.8 fusion.15
  392.0 3.5 copy.54
  395.5 3.8 reshape.191
  399.2 22.0 %all_to_all.36 = f32[2,1,186624]{2,1,0:T(1,128)S(1)} all-to-all(f32[2,1,186624]{2,1,0:T(1,128)} %reshape.191), channel_id=1, replica_groups=mesh['band'=16,'fft'=2] {'fft'}, dimensions={0} | all-to-all | bytes 2985984 | tf_op jit(solution)/shard_map/all_to_all | solution.py:80
  421.8 6.2 %reduce = f32[2,186624]{1,0:T(2,128)} reduce(f32[2,1,186624]{2,1,0:T(1,128)S(1)} %all_to_all.36, f32[]{:T(128)} %broadcast.120), dimensions={1}, to_apply=%all_to_all.30.reduce_sub_computation | reduce | bytes 2985988 | tf_op jit(solution)/shard_map/all_to_all | solution.py:80
  428.0 4.1 reshape.192
  432.1 3.6 copy.72
  435.7 3.3 all_to_all.33
  439.0 5.8 %fusion.20 = f32[18,144,288]{2,1,0:T(8,128)} fusion(f32[144,18,144]{0,2,1:T(8,128)S(1)} %all_to_all.33, f32[288,144]{0,1:T(8,128)S(1)} %copy-done.2), kind=kOutput, calls=%fused_computation.37 | convolution fusion | flops 1290069504 | bytes 4644864 | tf_op jit(solution)/shard_map/rgf,hr->gfh/dot_general | solution.py:15
  (27 shorter events, 2.1 us)
Async XLA Ops:
  16.0 7.5 %copy-start.3 = (s32[5184]{0:T(1024)S(1)}, s32[5184]{0:T(1024)}, u32[]{:S(2)}) copy-start(s32[5184]{0:T(1024)} %param.4) | copy-start | bytes 62212
  19.3 41.3 %all-to-all-start = ((f32[1,2,144,2592]{3,1,0,2:T(2,128)}), f32[1,2,144,2592]{3,1,0,2:T(2,128)S(1)}, u32[]{:S(2)}, u32[]{:S(2)}) async-start(f32[1,2,144,2592]{3,1,0,2:T(2,128)} %copy.44), calls=%async_computation | async-start | bytes 6193152 | tf_op jit(solution)/shard_map/all_to_all | solution.py:61
  23.5 356.4 %all-reduce.2.cloned.1.call-start = ((), (), s32[]{:S(2)}) async-start(), calls=%async_computation.2 | async-start | bytes 21233664 | tf_op jit(solution)/shard_map/psum | solution.py:73
  140.9 11.7 %copy-start = (f32[72,72,144]{2,1,0:T(8,128)}, f32[72,72,144]{2,1,0:T(8,128)S(1)}, u32[]{:S(2)}) copy-start(f32[72,72,144]{2,1,0:T(8,128)S(1)} %fusion.14) | copy-start | bytes 8957956
  235.8 152.3 %copy-start.1 = (f32[288,144]{0,1:T(8,128)}, f32[288,144]{0,1:T(8,128)S(1)}, u32[]{:S(2)}) copy-start(f32[288,144]{0,1:T(8,128)S(1)} %fusion.3) | copy-start | bytes 497668
  435.7 3.3 copy-start.2
Sparse Core Ops, SparseCore 0:
  174.6 205.2 all-reduce.1
where the time goes:
time: 458 us; the launch traced here: 452 us
  waiting for transfers between devices  144 us (31%)
  matrix products  101 us (22%)
  local copies, waits for them, and re-layouts  92.8 us (20%)
  other arithmetic  73.2 us (16%)
  blocking collectives  22 us (5%)
  between operations  14.5 us (3%)
    psum x1, waiting for transfers between devices, local(): summed = lax.psum(partial_value, 'band')  144 us
    dot_general x15, matrix products, product(): jnp.einsum(pattern, operand_a, operand_b, precision=lax.Precision.HIGHEST)  101 us
    reduce_sum x1, other arithmetic, interpolation_matrix(): return (1.0 + 2.0 * jnp.sum(jnp.cos(angles), axis=2)) / coarse_len  61.2 us
    scatter x1, local copies, waits for them, and re-layouts, local(): jnp.zeros((NCOLS,), jnp.int32).at[col_index]  36.3 us
    gather x2, local copies, waits for them, and re-layouts, local(): box_grid = jnp.take(block_in, inverse, axis=3)  27.5 us
    all_to_all x1, blocking collectives, local(): lax.all_to_all(reduced, 'fft', split_axis=2, concat_axis=0, tiled=True)  22 us
  transfers between devices with their start and end apart: 2, of which 1 were waited for; matrix products, arithmetic and copies ran while one was open for 22% of the time, Pallas kernels for 0%

commit v1 on v0

v1 whole, which is shorter than its diff:
```python
import math

import jax
import jax.numpy as jnp
import numpy as np
from jax import lax
from jax.experimental import pallas as pl
from jax.experimental.pallas import tpu as pltpu
from jax.sharding import PartitionSpec as P

NC = 144
NF = 288
KZ = 72
NCOLS = KZ * KZ
LANES = 128
MESH = pl.DeviceIdType.MESH


def product(pattern, operand_a, operand_b):
    return jnp.einsum(pattern, operand_a, operand_b, precision=lax.Precision.HIGH)


def round_up(size, unit):
    return -(-size // unit) * unit


def phase_tables():
    wave = np.arange(KZ) - KZ // 2
    angles = np.mod(np.arange(NC)[:, None] * wave[None, :], NC) * (2.0 * math.pi / NC)
    return np.cos(angles), np.sin(angles)


def interpolation_matrix():
    offsets = np.arange(NF)[:, None] - 2 * np.arange(NC)[None, :]
    waves = np.arange(1, NC // 2)
    angles = np.mod(offsets[:, :, None] * waves, NF) * (2.0 * math.pi / NF)
    return ((1.0 + 2.0 * np.sum(np.cos(angles), axis=2)) / NC).astype(np.float32)


def line_table(planes_padded):
    cos_t, sin_t = phase_tables()
    table = np.zeros((planes_padded, 2, 2, KZ), np.float32)
    table[:NC, 0, 0], table[:NC, 0, 1] = cos_t, -sin_t
    table[:NC, 1, 0], table[:NC, 1, 1] = sin_t, cos_t
    return table


def split_table():
    cos_t, sin_t = phase_tables()
    table = np.concatenate([cos_t, sin_t], axis=0).astype(np.float32)
    high = table.astype(jnp.bfloat16)
    low = (table - high.astype(np.float32)).astype(jnp.bfloat16)
    return np.concatenate([high, high, low], axis=1)


def exchange_kernel(src, dst, send_sem, recv_sem, local_sem):
    fft_size = lax.axis_size("fft")
    total = lax.axis_size("band") * fft_size
    me = lax.axis_index("band") * fft_size + lax.axis_index("fft")
    barrier = pltpu.get_barrier_semaphore()
    targets = []
    for step in range(1, total):
        target = lax.rem(me + step, total)
        targets.append((target, (target // fft_size, lax.rem(target, fft_size))))
        pl.semaphore_signal(barrier, inc=1, device_id=targets[-1][1], device_id_type=MESH)
    own = pltpu.make_async_copy(src.at[me], dst.at[me], local_sem)
    own.start()
    pl.semaphore_wait(barrier, total - 1)
    copies = []
    for step in range(1, total):
        target, device = targets[step - 1]
        copy = pltpu.make_async_remote_copy(
            src_ref=src.at[target],
            dst_ref=dst.at[me],
            send_sem=send_sem.at[step],
            recv_sem=recv_sem.at[step],
            device_id=device,
            device_id_type=MESH,
        )
        copy.start()
        copies.append(copy)
    own.wait()
    for copy in copies:
        copy.wait()


def exchange(blocks, collective_id):
    total = blocks.shape[0]
    return pl.pallas_call(
        exchange_kernel,
        out_shape=jax.ShapeDtypeStruct(blocks.shape, blocks.dtype),
        in_specs=[pl.BlockSpec(memory_space=pl.ANY)],
        out_specs=pl.BlockSpec(memory_space=pl.ANY),
        scratch_shapes=[
            pltpu.SemaphoreType.DMA((total,)),
            pltpu.SemaphoreType.DMA((total,)),
            pltpu.SemaphoreType.DMA,
        ],
        compiler_params=pltpu.CompilerParams(collective_id=collective_id, has_side_effects=True),
        name=f"exchange{collective_id}",
    )(blocks)


def split_rows(data):
    high = data.astype(jnp.bfloat16).astype(jnp.float32)
    return jnp.concatenate([high, data - high, high], axis=0).astype(jnp.bfloat16)


def plane_kernel(cols, columns, index, table, pick, out, rows, box, half_re, half_im):
    parts, _, lanes, cols_padded = columns.shape
    for part in range(parts):
        def turn(block, carry):
            at = pl.multiple_of(block * LANES, LANES)
            for which in range(2):
                rows[pl.ds(part * cols_padded + at, LANES), pl.ds(which * lanes, lanes)] = columns[
                    part, which, :, pl.ds(at, LANES)
                ].T
            return carry

        lax.fori_loop(0, cols_padded // LANES, turn, 0)

    unroll = math.gcd(cols, 8)
    for part in range(parts):
        def place(step, carry):
            for lane in range(unroll):
                col = step * unroll + lane
                box[pl.ds(index[part * cols + col], 1), :] = rows[
                    pl.ds(part * cols_padded + col, 1), :
                ]
            return carry

        lax.fori_loop(0, cols // unroll, place, 0)

    def rotate(stacked):
        full = jnp.dot(table[...], stacked, preferred_element_type=jnp.float32)
        real = full[:NC, :lanes] - full[NC:, lanes:]
        imag = full[NC:, :lanes] + full[:NC, lanes:]
        return real, imag

    def second(first, carry):
        data = box[pl.ds(pl.multiple_of(first * KZ, 8), KZ), :]
        real, imag = rotate(split_rows(data))
        at = pl.ds(pl.multiple_of(first * NC, 8), NC)
        half_re[at, :] = real
        half_im[at, :] = imag
        return carry

    lax.fori_loop(0, KZ, second, 0)

    def third(point, carry):
        at = pl.ds(point, KZ, stride=NC)
        data = jnp.concatenate([half_re[at, :], half_im[at, :]], axis=1)
        real, imag = rotate(split_rows(data))
        moduli = real * real + imag * imag
        high = moduli.astype(jnp.bfloat16)
        low = (moduli - high.astype(jnp.float32)).astype(jnp.bfloat16)
        both = jnp.concatenate([high, low], axis=1)
        out[point] = lax.dot_general(
            pick[...], both, (((1,), (1,)), ((), ())), preferred_element_type=jnp.float32
        )
        return carry

    lax.fori_loop(0, NC, third, 0)


def local(coefficients, col_index, occupation):
    band_here, _, _, cols = coefficients.shape
    band_size, fft_size = lax.axis_size("band"), lax.axis_size("fft")
    total = band_size * fft_size
    bands = band_here * band_size
    planes = -(-NC // total)
    radius = KZ // 2
    local_cols = lax.dynamic_slice_in_dim(col_index, lax.axis_index("fft") * cols, cols)
    first_wave = local_cols // KZ - radius
    second_wave = local_cols % KZ - radius
    third_wave = jnp.arange(KZ, dtype=jnp.int32) - radius
    radial = (first_wave * first_wave + second_wave * second_wave)[None, :] + (
        third_wave * third_wave
    )[:, None]
    inside = (radial <= radius * radius).astype(jnp.float32)
    amplitude = jnp.sqrt(occupation.astype(jnp.float32) / bands)
    masked = coefficients * inside * amplitude[:, None, None, None]

    table = jnp.asarray(line_table(total * planes))
    lines = product("zpqk,bqkc->zbpc", table, masked)
    lines = lines.reshape(total, planes * band_here, 2, cols)
    lines = exchange(lines, 0)

    columns = lines.reshape(band_size, fft_size, planes * band_here, 2, cols)
    columns = columns.transpose(1, 3, 0, 2, 4).reshape(fft_size, 2, band_size * planes * band_here, cols)
    lane_count = band_size * planes * band_here
    lanes = round_up(lane_count, LANES)
    cols_padded = round_up(cols, LANES)
    columns = jnp.pad(columns, ((0, 0), (0, 0), (0, lanes - lane_count), (0, cols_padded - cols)))

    plane_rows = round_up(planes, 8)
    pick = np.zeros((plane_rows, lanes), np.float32)
    lane = np.arange(lane_count)
    pick[(lane // band_here) % planes, lane] = 1.0
    pick = jnp.asarray(np.concatenate([pick, pick], axis=1), jnp.bfloat16)

    vmem = pl.BlockSpec(memory_space=pltpu.VMEM)
    density = pl.pallas_call(
        lambda *refs: plane_kernel(cols, *refs),
        out_shape=jax.ShapeDtypeStruct((NC, plane_rows, NC), jnp.float32),
        in_specs=[vmem, pl.BlockSpec(memory_space=pltpu.SMEM), vmem, vmem],
        out_specs=vmem,
        scratch_shapes=[
            pltpu.VMEM((fft_size * cols_padded, 2 * lanes), jnp.float32),
            pltpu.VMEM((NCOLS, 2 * lanes), jnp.float32),
            pltpu.VMEM((KZ * NC, lanes), jnp.float32),
            pltpu.VMEM((KZ * NC, lanes), jnp.float32),
        ],
        compiler_params=pltpu.CompilerParams(vmem_limit_bytes=56 * 1024 * 1024),
        name="planes",
    )(columns, col_index, jnp.asarray(split_table()), pick)

    interpolation = jnp.asarray(interpolation_matrix())
    row_share = NF // band_size
    wide = product("ga,bza->gzb", interpolation, density[:, :planes])
    chunk = row_share * planes * NC
    chunk_padded = round_up(chunk, 8 * LANES)
    wide = jnp.pad(wide.reshape(band_size, chunk), ((0, 0), (0, chunk_padded - chunk)))
    wide = wide.reshape(band_size, 1, chunk_padded // LANES, LANES)
    wide = jnp.broadcast_to(wide, (band_size, fft_size) + wide.shape[2:])
    wide = exchange(wide.reshape(total, chunk_padded // LANES, LANES), 1)
    wide = wide.reshape(total, chunk_padded)[:, :chunk].reshape(total, row_share, planes, NC)

    col_share = NF // fft_size
    own = lax.dynamic_slice_in_dim(interpolation, lax.axis_index("fft") * col_share, col_share, 0)
    full = product("tgpb,fb->gftp", wide, own).reshape(row_share, col_share, total * planes)
    last = jnp.asarray(np.pad(interpolation_matrix(), ((0, 0), (0, total * planes - NC))))
    return product("gfz,hz->gfh", full, last)


def solution(mesh):
    return jax.shard_map(
        local,
        mesh=mesh,
        in_specs=(P("band", None, None, "fft"), P(), P("band")),
        out_specs=P("band", "fft", None),
        check_vma=False,
    )
```

time: 458 us -> 262 us (0.57)
  the two profiles are of different devices: /device:TPU:0 before, /device:TPU:15 now
where the time goes in v1:
time: 262 us
  Pallas kernels  223 us (85%)
  local copies, waits for them, and re-layouts  21.2 us (8%)
  matrix products  15.9 us (6%)
    pallas_call x2, Pallas kernels, exchange(): pl.pallas_call(exchange_kernel, out_shape=jax.ShapeDtypeStruct(blocks.sha...  127 us
    pallas_call x1, Pallas kernels, local(): pl.pallas_call(lambda *refs: plane_kernel(cols, *refs), out_shape=jax.Sha...  96.1 us
    dot_general x4, matrix products, product(): jnp.einsum(pattern, operand_a, operand_b, precision=lax.Precision.HIGH)  15.9 us
    transpose x3, local copies, waits for them, and re-layouts, product(): jnp.einsum(pattern, operand_a, operand_b, precision=lax.Precision.HIGH)  7.46 us

profile of v1, /device:TPU:15, one launch (start us, length us, event | category | flops | bytes accessed | tf_op | source)
XLA Modules:
  0.0 261.8 jit_solution(1092089295191510740)
XLA Ops:
  0.7 0.8 fusion.18
  1.5 0.1 fusion.12
  1.7 3.2 %convolution_bitcast_fusion = f32[160,1,2,2592]{3,0,2,1:T(8,128)S(1)} fusion(f32[160,2,2,72]{0,3,2,1:T(8,128)} %constant.56.clone, f32[1,2,72,2592]{3,2,1,0:T(8,128)} %param.8, f32[]{:T(128)} %bitcast.1, f32[72,2592]{1,0:T(8,128)S(1)} %fusion.12), kind=kOutput, calls=%fused_computation | convolution fusion | flops 717382656 | bytes 5741572 | tf_op jit(solution)/shard_map/zpqk,bqkc->zbpc/dot_general | solution.py:20
  4.9 4.4 %copy.13 = f32[160,1,2,2592]{3,2,0,1:T(2,128)} copy(f32[160,1,2,2592]{3,0,2,1:T(8,128)S(1)} %convolution_bitcast_fusion) | data formatting | bytes 6635520 | tf_op jit(solution)/shard_map/zpqk,bqkc->zbpc/transpose | solution.py:20
  9.3 83.4 %exchange0.1 = f32[32,5,2,2592]{3,2,1,0:T(2,128)} custom-call(f32[32,5,2,2592]{3,2,1,0:T(2,128)} %bitcast.38), custom_call_target="tpu_custom_call" | custom-call | tf_op jit(solution)/shard_map/exchange0/pallas_call | solution.py:89
  92.6 3.2 %copy.14 = f32[16,2,5,2,2592]{4,3,2,0,1:T(2,128)S(1)} copy(f32[16,2,5,2,2592]{4,3,2,1,0:T(2,128)} %bitcast.39) | data formatting | bytes 6635520 | tf_op jit(solution)/shard_map/reshape | solution.py:189
  95.8 0.2 copy.15
  96.0 2.8 %pad.8.refs_0_ = f32[2,2,128,2688]{3,2,1,0:T(8,128)} pad(f32[2,2,80,2592]{3,2,1,0:T(8,128)S(1)} %copy.15, f32[]{:T(128)} %constant.55.clone.1), padding=0_0x0_0x0_48x0_96 | pad | bytes 8822788 | tf_op jit(solution)/shard_map/jit(_pad)/pad | solution.py:194
  98.8 0.0 copy-start.1
  98.8 96.1 %planes.1 = f32[144,8,144]{2,1,0:T(8,128)} custom-call(f32[2,2,128,2688]{3,2,1,0:T(8,128)} %pad.8.refs_0_, s32[5184]{0:T(1024)} %refs_1_.1, bf16[288,216]{1,0:T(8,128)(2,1)} %constant.58.clone.refs_2_, bf16[8,256]{1,0:T(8,128)(2,1)} %constant.57.clone.refs_3_), custom_call_target="tpu_custom_call" | custom-call | tf_op jit(solution)/shard_map/planes/pallas_call | solution.py:203
  194.9 0.0 copy-done.1
  194.9 2.1 convolution_bitcast_fusion.1
  197.0 1.3 copy.17
  198.3 0.7 reshape.74
  199.0 0.1 pad_bitcast_fusion
  199.1 0.2 copy.25
  199.2 1.3 broadcast_in_dim.5
  200.5 43.4 %exchange1.1 = f32[32,104,128]{2,1,0:T(8,128)} custom-call(f32[32,104,128]{2,1,0:T(8,128)} %bitcast.42), custom_call_target="tpu_custom_call" | custom-call | tf_op jit(solution)/shard_map/exchange1/pallas_call | solution.py:89
  243.9 1.8 copy.36
  245.7 0.1 slice.9
  245.8 0.0 copy-start.2
  245.8 3.5 %reshape.77 = f32[32,18,5,144]{3,2,1,0:T(8,128)} reshape(f32[32,12960]{1,0:T(8,128)S(1)} %slice.9) | data formatting | bytes 3317760 | tf_op jit(solution)/shard_map/reshape | solution.py:227
  249.3 0.0 copy-done.2
  249.3 5.3 %fusion.4 = f32[18,144,32,5]{1,2,3,0:T(8,128)S(1)} fusion(f32[32,18,5,144]{3,2,1,0:T(8,128)} %reshape.77, f32[288,144]{0,1:T(8,128)S(1)} %copy-done.2, s32[]{:T(128)S(6)} %select_n.18), kind=kOutput, calls=%fused_computation.5 | convolution fusion | flops 358318080 | bytes 3465220 | tf_op jit(solution)/shard_map/tgpb,fb->gftp/dot_general | solution.py:20
  254.6 0.0 copy-start
  254.7 1.8 copy.20
  256.4 0.0 copy-done
  256.4 5.4 %fusion = f32[18,144,288]{2,1,0:T(8,128)} fusion(f32[288,160,1]{0,1,2:T(8,128)S(1)} %copy-done, f32[18,144,160]{1,0,2:T(8,128)S(1)} %bitcast.41), kind=kOutput, calls=%fused_computation.1 | convolution fusion | flops 716636160 | bytes 4829184 | tf_op jit(solution)/shard_map/gfz,hz->gfh/dot_general | solution.py:20
  (1 shorter events, 0.0 us)
Async XLA Ops:
  98.8 96.1 %copy-start.1 = (f32[288,144,1]{0,1,2:T(8,128)S(1)}, f32[288,144,1]{0,1,2:T(8,128)}, u32[]{:S(2)}) copy-start(f32[288,144,1]{0,1,2:T(8,128)} %constant.67) | copy-start | bytes 497668
  245.8 3.6 %copy-start.2 = (f32[288,144]{0,1:T(8,128)S(1)}, f32[288,144]{0,1:T(8,128)}, u32[]{:S(2)}) copy-start(f32[288,144]{0,1:T(8,128)} %constant.59.clone) | copy-start | bytes 497668
  254.6 1.8 copy-start

commit v2 on v1

--- a/solution.py
+++ b/solution.py
@@ -13,6 +13,8 @@
 KZ = 72
 NCOLS = KZ * KZ
 LANES = 128
+FOLD_WAVES = 40
+FOLD_POINTS = 80
 MESH = pl.DeviceIdType.MESH
 
 
@@ -45,12 +47,29 @@
     return table
 
 
-def split_table():
-    cos_t, sin_t = phase_tables()
-    table = np.concatenate([cos_t, sin_t], axis=0).astype(np.float32)
-    high = table.astype(jnp.bfloat16)
-    low = (table - high.astype(np.float32)).astype(jnp.bfloat16)
-    return np.concatenate([high, high, low], axis=1)
+def fold_tables():
+    half = KZ // 2
+    points = np.arange(NC // 2 + 1)
+    waves = np.concatenate([np.arange(half), [half]])
+    angles = np.mod(points[:, None] * waves[None, :], NC) * (2.0 * math.pi / NC)
+    tables = []
+    for values in (np.cos(angles), np.sin(angles)):
+        table = np.zeros((FOLD_POINTS, FOLD_WAVES), np.float32)
+        table[: NC // 2 + 1, : half + 1] = values
+        high = table.astype(jnp.bfloat16)
+        low = (table - high.astype(np.float32)).astype(jnp.bfloat16)
+        tables.append(np.concatenate([high, high, low], axis=1))
+    return np.stack(tables)
+
+
+def fold_slots():
+    points = np.arange(NC)
+    return np.where(points <= NC // 2, points, FOLD_POINTS + NC - points)
+
+
+def wave_slots(index):
+    half = KZ // 2
+    return jnp.where(index >= half, index - half, jnp.where(index == 0, half, KZ - index))
 
 
 def exchange_kernel(src, dst, send_sem, recv_sem, local_sem):
@@ -131,26 +150,43 @@
 
         lax.fori_loop(0, cols // unroll, place, 0)
 
-    def rotate(stacked):
-        full = jnp.dot(table[...], stacked, preferred_element_type=jnp.float32)
-        real = full[:NC, :lanes] - full[NC:, lanes:]
-        imag = full[NC:, :lanes] + full[:NC, lanes:]
+    half = KZ // 2
+    single = lax.broadcasted_iota(jnp.int32, (half + 4, 2 * lanes), 0)[:half] == 0
+    last_row = lax.broadcasted_iota(jnp.int32, (8, 2 * lanes), 0)[: FOLD_WAVES - half] == 0
+
+    def rotate(ahead, behind):
+        alone = jnp.where(last_row, jnp.broadcast_to(behind[:1], last_row.shape), 0.0)
+        behind = jnp.where(single, 0.0, behind)
+        even = jnp.concatenate([ahead + behind, alone], axis=0)
+        odd = jnp.concatenate([ahead - behind, -alone], axis=0)
+        cos_part = jnp.dot(table[0], split_rows(even), preferred_element_type=jnp.float32)
+        sin_part = jnp.dot(table[1], split_rows(odd), preferred_element_type=jnp.float32)
+        cos_re, cos_im = cos_part[:, :lanes], cos_part[:, lanes:]
+        sin_re, sin_im = sin_part[:, :lanes], sin_part[:, lanes:]
+        real = jnp.concatenate([cos_re - sin_im, cos_re + sin_im], axis=0)
+        imag = jnp.concatenate([cos_im + sin_re, cos_im - sin_re], axis=0)
         return real, imag
 
+    slots = 2 * FOLD_POINTS
+
     def second(first, carry):
-        data = box[pl.ds(pl.multiple_of(first * KZ, 8), KZ), :]
-        real, imag = rotate(split_rows(data))
-        at = pl.ds(pl.multiple_of(first * NC, 8), NC)
+        at = pl.multiple_of(first * KZ, 8)
+        data = box[pl.ds(at, KZ), :]
+        real, imag = rotate(data[:half], data[half:])
+        at = pl.ds(pl.multiple_of(first * slots, 8), slots)
         half_re[at, :] = real
         half_im[at, :] = imag
         return carry
 
-    lax.fori_loop(0, KZ, second, 0)
+    lax.fori_loop(0, KZ, second, 0, unroll=4)
 
     def third(point, carry):
-        at = pl.ds(point, KZ, stride=NC)
-        data = jnp.concatenate([half_re[at, :], half_im[at, :]], axis=1)
-        real, imag = rotate(split_rows(data))
+        slot = jnp.where(point <= NC // 2, point, point + FOLD_POINTS - NC // 2)
+        parts = []
+        for base in (0, half):
+            at = pl.ds(slot + base * slots, half, stride=slots)
+            parts.append(jnp.concatenate([half_re[at, :], half_im[at, :]], axis=1))
+        real, imag = rotate(*parts)
         moduli = real * real + imag * imag
         high = moduli.astype(jnp.bfloat16)
         low = (moduli - high.astype(jnp.float32)).astype(jnp.bfloat16)
@@ -160,7 +196,7 @@
         )
         return carry
 
-    lax.fori_loop(0, NC, third, 0)
+    lax.fori_loop(0, NC, third, 0, unroll=4)
 
 
 def local(coefficients, col_index, occupation):
@@ -199,25 +235,27 @@
     pick[(lane // band_here) % planes, lane] = 1.0
     pick = jnp.asarray(np.concatenate([pick, pick], axis=1), jnp.bfloat16)
 
+    places = wave_slots(col_index // KZ) * KZ + wave_slots(col_index % KZ)
     vmem = pl.BlockSpec(memory_space=pltpu.VMEM)
     density = pl.pallas_call(
         lambda *refs: plane_kernel(cols, *refs),
-        out_shape=jax.ShapeDtypeStruct((NC, plane_rows, NC), jnp.float32),
+        out_shape=jax.ShapeDtypeStruct((NC, plane_rows, 2 * FOLD_POINTS), jnp.float32),
         in_specs=[vmem, pl.BlockSpec(memory_space=pltpu.SMEM), vmem, vmem],
         out_specs=vmem,
         scratch_shapes=[
             pltpu.VMEM((fft_size * cols_padded, 2 * lanes), jnp.float32),
             pltpu.VMEM((NCOLS, 2 * lanes), jnp.float32),
-            pltpu.VMEM((KZ * NC, lanes), jnp.float32),
-            pltpu.VMEM((KZ * NC, lanes), jnp.float32),
+            pltpu.VMEM((KZ * 2 * FOLD_POINTS, lanes), jnp.float32),
+            pltpu.VMEM((KZ * 2 * FOLD_POINTS, lanes), jnp.float32),
         ],
         compiler_params=pltpu.CompilerParams(vmem_limit_bytes=56 * 1024 * 1024),
         name="planes",
-    )(columns, col_index, jnp.asarray(split_table()), pick)
-
-    interpolation = jnp.asarray(interpolation_matrix())
+    )(columns, places, jnp.asarray(fold_tables()), pick)
+
     row_share = NF // band_size
-    wide = product("ga,bza->gzb", interpolation, density[:, :planes])
+    first_table = np.zeros((NF, 2 * FOLD_POINTS), np.float32)
+    first_table[:, fold_slots()] = interpolation_matrix()
+    wide = product("ga,bza->gzb", jnp.asarray(first_table), density[:, :planes])
     chunk = row_share * planes * NC
     chunk_padded = round_up(chunk, 8 * LANES)
     wide = jnp.pad(wide.reshape(band_size, chunk), ((0, 0), (0, chunk_padded - chunk)))
@@ -227,6 +265,8 @@
     wide = wide.reshape(total, chunk_padded)[:, :chunk].reshape(total, row_share, planes, NC)
 
     col_share = NF // fft_size
+    order = np.concatenate([np.arange(NC // 2 + 1), np.arange(NC - 1, NC // 2, -1)])
+    interpolation = jnp.asarray(interpolation_matrix()[:, order])
     own = lax.dynamic_slice_in_dim(interpolation, lax.axis_index("fft") * col_share, col_share, 0)
     full = product("tgpb,fb->gftp", wide, own).reshape(row_share, col_share, total * planes)
     last = jnp.asarray(np.pad(interpolation_matrix(), ((0, 0), (0, total * planes - NC))))

time: 262 us -> 221 us (0.84)
  Pallas kernels: 223 us -> 181 us
    pallas_call x1, Pallas kernels: 96.1 us -> 54.7 us  [local(): pl.pallas_call(lambda *refs: plane_kernel(cols, *refs), out_shape=jax.Sha...]
where the time goes in v2:
time: 221 us
  Pallas kernels  181 us (82%)
  local copies, waits for them, and re-layouts  21.2 us (10%)
  matrix products  15.9 us (7%)
    pallas_call x2, Pallas kernels, exchange(): pl.pallas_call(exchange_kernel, out_shape=jax.ShapeDtypeStruct(blocks.sha...  127 us
    pallas_call x1, Pallas kernels, local(): pl.pallas_call(lambda *refs: plane_kernel(cols, *refs), out_shape=jax.Sha...  54.7 us
    dot_general x4, matrix products, product(): jnp.einsum(pattern, operand_a, operand_b, precision=lax.Precision.HIGH)  15.9 us
    transpose x3, local copies, waits for them, and re-layouts, product(): jnp.einsum(pattern, operand_a, operand_b, precision=lax.Precision.HIGH)  7.46 us

profile of v2, /device:TPU:15, one launch (start us, length us, event | category | flops | bytes accessed | tf_op | source)
XLA Modules:
  0.0 220.8 jit_solution(12717741697712815580)
XLA Ops:
  0.0 0.8 fusion.19
  0.8 0.1 fusion.12
  1.7 3.2 %convolution_bitcast_fusion = f32[160,1,2,2592]{3,0,2,1:T(8,128)S(1)} fusion(f32[160,2,2,72]{0,3,2,1:T(8,128)} %constant.76.clone, f32[1,2,72,2592]{3,2,1,0:T(8,128)} %param.9, f32[]{:T(128)} %bitcast.2, f32[72,2592]{1,0:T(8,128)S(1)} %fusion.12), kind=kOutput, calls=%fused_computation | convolution fusion | flops 717382656 | bytes 5741572 | tf_op jit(solution)/shard_map/zpqk,bqkc->zbpc/dot_general | solution.py:22
  4.8 4.4 %copy.13 = f32[160,1,2,2592]{3,2,0,1:T(2,128)} copy(f32[160,1,2,2592]{3,0,2,1:T(8,128)S(1)} %convolution_bitcast_fusion) | data formatting | bytes 6635520 | tf_op jit(solution)/shard_map/zpqk,bqkc->zbpc/transpose | solution.py:22
  9.3 83.4 %exchange0.1 = f32[32,5,2,2592]{3,2,1,0:T(2,128)} custom-call(f32[32,5,2,2592]{3,2,1,0:T(2,128)} %bitcast.40), custom_call_target="tpu_custom_call" | custom-call | tf_op jit(solution)/shard_map/exchange0/pallas_call | solution.py:108
  92.6 3.2 %copy.14 = f32[16,2,5,2,2592]{4,3,2,0,1:T(2,128)S(1)} copy(f32[16,2,5,2,2592]{4,3,2,1,0:T(2,128)} %bitcast.41) | data formatting | bytes 6635520 | tf_op jit(solution)/shard_map/reshape | solution.py:225
  95.8 0.2 copy.15
  96.0 0.0 copy-start.3
  96.0 2.8 %pad.8.refs_0_ = f32[2,2,128,2688]{3,2,1,0:T(8,128)} pad(f32[2,2,80,2592]{3,2,1,0:T(8,128)S(1)} %copy.15, f32[]{:T(128)} %constant.74.clone.1), padding=0_0x0_0x0_48x0_96 | pad | bytes 8822788 | tf_op jit(solution)/shard_map/jit(_pad)/pad | solution.py:230
  98.8 0.0 copy-done.3
  98.8 0.6 select_add_fusion.refs_1_
  99.4 0.0 copy-start.1
  99.4 54.7 %planes.1 = f32[144,8,160]{2,1,0:T(8,128)} custom-call(f32[2,2,128,2688]{3,2,1,0:T(8,128)} %pad.8.refs_0_, s32[5184]{0:T(1024)} %select_add_fusion.refs_1_, bf16[2,80,120]{2,1,0:T(8,128)(2,1)} %constant.78.clone.refs_2_, bf16[8,256]{1,0:T(8,128)(2,1)} %constant.77.clone.refs_3_), custom_call_target="tpu_custom_call" | custom-call | tf_op jit(solution)/shard_map/planes/pallas_call | solution.py:240
  154.1 0.0 copy-done.1
  154.1 2.1 convolution_bitcast_fusion.1
  156.2 1.3 copy.17
  157.5 0.7 reshape.74
  158.2 0.1 pad_bitcast_fusion
  158.2 0.2 copy.23
  158.4 1.3 broadcast_in_dim.8
  159.7 43.2 %exchange1.1 = f32[32,104,128]{2,1,0:T(8,128)} custom-call(f32[32,104,128]{2,1,0:T(8,128)} %bitcast.44), custom_call_target="tpu_custom_call" | custom-call | tf_op jit(solution)/shard_map/exchange1/pallas_call | solution.py:108
  202.9 1.8 copy.34
  204.7 0.1 slice.9
  204.8 0.0 copy-start.2
  204.8 3.5 %reshape.77 = f32[32,18,5,144]{3,2,1,0:T(8,128)} reshape(f32[32,12960]{1,0:T(8,128)S(1)} %slice.9) | data formatting | bytes 3317760 | tf_op jit(solution)/shard_map/reshape | solution.py:265
  208.4 0.0 copy-done.2
  208.4 5.3 %fusion.4 = f32[18,144,32,5]{1,2,3,0:T(8,128)S(1)} fusion(f32[32,18,5,144]{3,2,1,0:T(8,128)} %reshape.77, f32[288,144]{1,0:T(8,128)S(1)} %copy-done.2, s32[]{:T(128)S(6)} %select_n.42), kind=kOutput, calls=%fused_computation.5 | convolution fusion | flops 358318080 | bytes 3465220 | tf_op jit(solution)/shard_map/tgpb,fb->gftp/dot_general | solution.py:22
  213.6 0.0 copy-start
  213.6 1.8 copy.19
  215.4 0.0 copy-done
  215.4 5.4 %fusion = f32[18,144,288]{2,1,0:T(8,128)} fusion(f32[288,160,1]{0,1,2:T(8,128)S(1)} %copy-done, f32[18,144,160]{1,0,2:T(8,128)S(1)} %bitcast.43), kind=kOutput, calls=%fused_computation.1 | convolution fusion | flops 716636160 | bytes 4829184 | tf_op jit(solution)/shard_map/gfz,hz->gfh/dot_general | solution.py:22
  (1 shorter events, 0.0 us)
Async XLA Ops:
  96.0 2.8 %copy-start.3 = (s32[5184]{0:T(1024)S(1)}, s32[5184]{0:T(1024)}, u32[]{:S(2)}) copy-start(s32[5184]{0:T(1024)} %param.10) | copy-start | bytes 62212
  99.4 54.7 %copy-start.1 = (f32[288,160,1]{0,1,2:T(8,128)S(1)}, f32[288,160,1]{0,1,2:T(8,128)}, u32[]{:S(2)}) copy-start(f32[288,160,1]{0,1,2:T(8,128)} %constant.88) | copy-start | bytes 552964
  204.8 3.5 %copy-start.2 = (f32[288,144]{1,0:T(8,128)S(1)}, f32[288,144]{1,0:T(8,128)}, u32[]{:S(2)}) copy-start(f32[288,144]{1,0:T(8,128)} %constant.80.clone) | copy-start | bytes 497668
  213.6 1.8 copy-start

commit v3 on v2

--- a/solution.py
+++ b/solution.py
@@ -13,6 +13,7 @@
 KZ = 72
 NCOLS = KZ * KZ
 LANES = 128
+LAYERS = 4
 FOLD_WAVES = 40
 FOLD_POINTS = 80
 MESH = pl.DeviceIdType.MESH
@@ -62,25 +63,34 @@
     return np.stack(tables)
 
 
-def fold_slots():
-    points = np.arange(NC)
-    return np.where(points <= NC // 2, points, FOLD_POINTS + NC - points)
-
-
 def wave_slots(index):
     half = KZ // 2
     return jnp.where(index >= half, index - half, jnp.where(index == 0, half, KZ - index))
 
 
-def exchange_kernel(src, dst, send_sem, recv_sem, local_sem):
-    fft_size = lax.axis_size("fft")
-    total = lax.axis_size("band") * fft_size
-    me = lax.axis_index("band") * fft_size + lax.axis_index("fft")
+def exchange_kernel(scope, src, dst, send_sem, recv_sem, local_sem):
+    band_size, fft_size = lax.axis_size("band"), lax.axis_size("fft")
+    band, fft = lax.axis_index("band"), lax.axis_index("fft")
+    layer = band_size // LAYERS
+    if scope == "all":
+        total, me = band_size * fft_size, band * fft_size + fft
+    elif scope == "layer":
+        total, me = layer * fft_size, lax.rem(band, layer) * fft_size + fft
+    else:
+        total, me = LAYERS, band // layer
+
+    def device_of(target):
+        if scope == "all":
+            return (target // fft_size, lax.rem(target, fft_size))
+        if scope == "layer":
+            return (band // layer * layer + target // fft_size, lax.rem(target, fft_size))
+        return (target * layer + lax.rem(band, layer), fft)
+
     barrier = pltpu.get_barrier_semaphore()
     targets = []
     for step in range(1, total):
         target = lax.rem(me + step, total)
-        targets.append((target, (target // fft_size, lax.rem(target, fft_size))))
+        targets.append((target, device_of(target)))
         pl.semaphore_signal(barrier, inc=1, device_id=targets[-1][1], device_id_type=MESH)
     own = pltpu.make_async_copy(src.at[me], dst.at[me], local_sem)
     own.start()
@@ -103,10 +113,10 @@
         copy.wait()
 
 
-def exchange(blocks, collective_id):
+def exchange(blocks, scope, collective_id):
     total = blocks.shape[0]
     return pl.pallas_call(
-        exchange_kernel,
+        lambda *refs: exchange_kernel(scope, *refs),
         out_shape=jax.ShapeDtypeStruct(blocks.shape, blocks.dtype),
         in_specs=[pl.BlockSpec(memory_space=pl.ANY)],
         out_specs=pl.BlockSpec(memory_space=pl.ANY),
@@ -116,7 +126,7 @@
             pltpu.SemaphoreType.DMA,
         ],
         compiler_params=pltpu.CompilerParams(collective_id=collective_id, has_side_effects=True),
-        name=f"exchange{collective_id}",
+        name=f"exchange_{scope}",
     )(blocks)
 
 
@@ -138,14 +148,14 @@
 
         lax.fori_loop(0, cols_padded // LANES, turn, 0)
 
-    unroll = math.gcd(cols, 8)
+    unroll = math.gcd(cols, 16)
     for part in range(parts):
         def place(step, carry):
-            for lane in range(unroll):
-                col = step * unroll + lane
-                box[pl.ds(index[part * cols + col], 1), :] = rows[
-                    pl.ds(part * cols_padded + col, 1), :
-                ]
+            first = step * unroll
+            batch = [rows[pl.ds(part * cols_padded + first + n, 1), :] for n in range(unroll)]
+            to = [index[part * cols + first + n] for n in range(unroll)]
+            for row, value in zip(to, batch):
+                box[pl.ds(row, 1), :] = value
             return carry
 
         lax.fori_loop(0, cols // unroll, place, 0)
@@ -204,7 +214,9 @@
     band_size, fft_size = lax.axis_size("band"), lax.axis_size("fft")
     total = band_size * fft_size
     bands = band_here * band_size
-    planes = -(-NC // total)
+    layer = band_size // LAYERS
+    group = layer * fft_size
+    planes = -(-NC // group)
     radius = KZ // 2
     local_cols = lax.dynamic_slice_in_dim(col_index, lax.axis_index("fft") * cols, cols)
     first_wave = local_cols // KZ - radius
@@ -217,14 +229,14 @@
     amplitude = jnp.sqrt(occupation.astype(jnp.float32) / bands)
     masked = coefficients * inside * amplitude[:, None, None, None]
 
-    table = jnp.asarray(line_table(total * planes))
+    table = jnp.asarray(line_table(group * planes))
     lines = product("zpqk,bqkc->zbpc", table, masked)
-    lines = lines.reshape(total, planes * band_here, 2, cols)
-    lines = exchange(lines, 0)
-
-    columns = lines.reshape(band_size, fft_size, planes * band_here, 2, cols)
-    columns = columns.transpose(1, 3, 0, 2, 4).reshape(fft_size, 2, band_size * planes * band_here, cols)
-    lane_count = band_size * planes * band_here
+    lines = lines.reshape(group, planes * band_here, 2, cols)
+    lines = exchange(lines, "layer", 0)
+
+    columns = lines.reshape(layer, fft_size, planes * band_here, 2, cols)
+    columns = columns.transpose(1, 3, 0, 2, 4).reshape(fft_size, 2, layer * planes * band_here, cols)
+    lane_count = layer * planes * band_here
     lanes = round_up(lane_count, LANES)
     cols_padded = round_up(cols, LANES)
     columns = jnp.pad(columns, ((0, 0), (0, 0), (0, lanes - lane_count), (0, cols_padded - cols)))
@@ -253,23 +265,39 @@
     )(columns, places, jnp.asarray(fold_tables()), pick)
 
     row_share = NF // band_size
-    first_table = np.zeros((NF, 2 * FOLD_POINTS), np.float32)
-    first_table[:, fold_slots()] = interpolation_matrix()
-    wide = product("ga,bza->gzb", jnp.asarray(first_table), density[:, :planes])
-    chunk = row_share * planes * NC
-    chunk_padded = round_up(chunk, 8 * LANES)
-    wide = jnp.pad(wide.reshape(band_size, chunk), ((0, 0), (0, chunk_padded - chunk)))
-    wide = wide.reshape(band_size, 1, chunk_padded // LANES, LANES)
-    wide = jnp.broadcast_to(wide, (band_size, fft_size) + wide.shape[2:])
-    wide = exchange(wide.reshape(total, chunk_padded // LANES, LANES), 1)
-    wide = wide.reshape(total, chunk_padded)[:, :chunk].reshape(total, row_share, planes, NC)
+    kept = NC // 2 + 1
+    density = density[:, :planes]
+    density = jnp.concatenate(
+        [density[..., :kept], density[..., FOLD_POINTS + 1 : FOLD_POINTS + 1 + NC - kept]], axis=2
+    )
+    points = NC // LAYERS
+
+    def exchange_flat(blocks, chunk, scope, collective_id):
+        padded = round_up(chunk, LANES)
+        flat = jnp.pad(blocks.reshape(-1, chunk), ((0, 0), (0, padded - chunk)))
+        flat = flat.reshape(-1, padded // LANES, LANES)
+        if scope == "all":
+            flat = jnp.broadcast_to(flat[:, None], (band_size, fft_size) + flat.shape[1:])
+            flat = flat.reshape((total,) + flat.shape[2:])
+        return exchange(flat, scope, collective_id)
+
+    part = exchange_flat(density, points * planes * NC, "column", 1)
+    summed = jnp.sum(part, axis=0).reshape(-1)[: points * planes * NC]
+    summed = summed.reshape(points, planes, NC)
+
+    order = np.concatenate([np.arange(kept), np.arange(NC - 1, kept - 1, -1)])
+    interpolation = jnp.asarray(interpolation_matrix()[:, order])
+    row_share = NF // band_size
+    wide = product("ga,pza->gzp", interpolation, summed)
+    chunk = row_share * planes * points
+    wide = exchange_flat(wide, chunk, "all", 2)
+    wide = wide.reshape(total, -1)[:, :chunk].reshape(LAYERS, group, row_share, planes, points)
 
     col_share = NF // fft_size
-    order = np.concatenate([np.arange(NC // 2 + 1), np.arange(NC - 1, NC // 2, -1)])
-    interpolation = jnp.asarray(interpolation_matrix()[:, order])
     own = lax.dynamic_slice_in_dim(interpolation, lax.axis_index("fft") * col_share, col_share, 0)
-    full = product("tgpb,fb->gftp", wide, own).reshape(row_share, col_share, total * planes)
-    last = jnp.asarray(np.pad(interpolation_matrix(), ((0, 0), (0, total * planes - NC))))
+    wide = wide.transpose(2, 1, 3, 0, 4).reshape(row_share, group * planes, NC)
+    full = product("gzb,fb->gfz", wide, own)
+    last = jnp.asarray(np.pad(interpolation_matrix(), ((0, 0), (0, group * planes - NC))))
     return product("gfz,hz->gfh", full, last)
 
 

time: 221 us -> 229 us (1.036)
  local copies, waits for them, and re-layouts: 21.2 us -> 43.9 us
  Pallas kernels: 181 us -> 167 us
  matrix products: 15.9 us -> 12.1 us
  other arithmetic: 1.6 us -> 4.84 us
    pallas_call x2 -> x3, Pallas kernels: 127 us -> 112 us  [exchange(): pl.pallas_call(lambda *refs: exchange_kernel(scope, *refs), out_shape=jax...]
    reshape x3 -> x5, local copies, waits for them, and re-layouts: 7.37 us -> 17.1 us  [the longest x1 5.08 us: local(): wide.reshape(total, -1)[:, :chunk]]
    transpose x0 -> x1, local copies, waits for them, and re-layouts: none -> 8.76 us  [local(): wide = wide.transpose(2, 1, 3, 0, 4).reshape(row_share, group * planes, NC)]
    dot_general x4, matrix products: 15.9 us -> 12.1 us  [product(): jnp.einsum(pattern, operand_a, operand_b, precision=lax.Precision.HIGH)]
    slice x1 -> x2, local copies, waits for them, and re-layouts: 0.11 us -> 2.78 us  [the longest x1 2.67 us: local(): density[..., FOLD_POINTS + 1:FOLD_POINTS + 1 + NC - kept]]
    transpose x3 -> x2, local copies, waits for them, and re-layouts: 7.46 us -> 6.52 us  [product(): jnp.einsum(pattern, operand_a, operand_b, precision=lax.Precision.HIGH)]
where the time goes in v3:
time: 229 us
  Pallas kernels  167 us (73%)
  local copies, waits for them, and re-layouts  43.9 us (19%)
  matrix products  12.1 us (5%)
  other arithmetic  4.84 us (2%)
    pallas_call x3, Pallas kernels, exchange(): pl.pallas_call(lambda *refs: exchange_kernel(scope, *refs), out_shape=jax...  112 us
    pallas_call x1, Pallas kernels, local(): pl.pallas_call(lambda *refs: plane_kernel(cols, *refs), out_shape=jax.Sha...  54.5 us
    dot_general x4, matrix products, product(): jnp.einsum(pattern, operand_a, operand_b, precision=lax.Precision.HIGH)  12.1 us
    transpose x1, local copies, waits for them, and re-layouts, local(): wide = wide.transpose(2, 1, 3, 0, 4).reshape(row_share, group * planes, NC)  8.76 us
    transpose x2, local copies, waits for them, and re-layouts, product(): jnp.einsum(pattern, operand_a, operand_b, precision=lax.Precision.HIGH)  6.52 us
    reshape x1, local copies, waits for them, and re-layouts, local(): wide.reshape(total, -1)[:, :chunk]  5.08 us

profile of v3, /device:TPU:15, one launch (start us, length us, event | category | flops | bytes accessed | tf_op | source)
XLA Modules:
  0.0 228.5 jit_solution(16195410951960130855)
XLA Ops:
  0.7 0.8 fusion.15
  1.5 1.4 select_add_fusion.refs_1_
  2.9 0.1 fusion.7
  3.1 3.0 %convolution_bitcast_fusion = f32[144,1,2,2592]{3,0,2,1:T(8,128)S(1)} fusion(f32[144,2,2,72]{3,0,2,1:T(8,128)} %constant.75.clone, f32[1,2,72,2592]{3,2,1,0:T(8,128)} %param.8, f32[]{:T(128)} %bitcast.1, f32[72,2592]{1,0:T(8,128)S(1)} %fusion.7), kind=kOutput, calls=%fused_computation | convolution fusion | flops 645719040 | bytes 5391364 | tf_op jit(solution)/shard_map/zpqk,bqkc->zbpc/dot_general | solution.py:23
  6.1 3.2 %copy.11 = f32[144,1,2,2592]{3,2,0,1:T(2,128)} copy(f32[144,1,2,2592]{3,0,2,1:T(8,128)S(1)} %convolution_bitcast_fusion) | data formatting | bytes 5971968 | tf_op jit(solution)/shard_map/zpqk,bqkc->zbpc/transpose | solution.py:23
  9.3 37.6 %exchange_layer.1 = f32[8,18,2,2592]{3,2,1,0:T(2,128)} custom-call(f32[8,18,2,2592]{3,2,1,0:T(2,128)} %bitcast.38), custom_call_target="tpu_custom_call" | custom-call | tf_op jit(solution)/shard_map/exchange_layer/pallas_call | solution.py:118
  46.9 2.9 %copy.12 = f32[4,2,18,2,2592]{4,3,2,0,1:T(2,128)S(1)} copy(f32[4,2,18,2,2592]{4,3,2,1,0:T(2,128)} %bitcast.39) | data formatting | bytes 5971968 | tf_op jit(solution)/shard_map/reshape | solution.py:237
  49.8 0.2 copy.13
  50.0 2.8 %pad.8.refs_0_ = f32[2,2,128,2688]{3,2,1,0:T(8,128)} pad(f32[2,2,72,2592]{3,2,1,0:T(8,128)S(1)} %copy.13, f32[]{:T(128)} %constant.73.clone.1), padding=0_0x0_0x0_56x0_96 | pad | bytes 8491012 | tf_op jit(solution)/shard_map/jit(_pad)/pad | solution.py:242
  52.8 54.5 %planes.1 = f32[144,24,160]{2,1,0:T(8,128)} custom-call(f32[2,2,128,2688]{3,2,1,0:T(8,128)} %pad.8.refs_0_, s32[5184]{0:T(1024)} %select_add_fusion.refs_1_, bf16[2,80,120]{2,1,0:T(8,128)(2,1)} %constant.77.clone.refs_2_, bf16[24,256]{1,0:T(8,128)(2,1)} %constant.76.clone.refs_3_), custom_call_target="tpu_custom_call" | custom-call | tf_op jit(solution)/shard_map/planes/pallas_call | solution.py:252
  107.2 2.7 %slice.16 = f32[144,18,71]{2,1,0:T(8,128)S(1)} slice(f32[144,24,160]{2,1,0:T(8,128)} %planes.1), slice={[0:144], [0:18], [81:152]} | slice | bytes 1472256 | tf_op jit(solution)/shard_map/slice | solution.py:271
  109.9 0.4 copy-done
  110.3 0.1 slice.15
  110.4 1.0 pad_maximum_fusion
  111.4 2.8 %reshape.78.refs_0_ = f32[4,729,128]{2,1,0:T(8,128)} reshape(f32[144,18,144]{2,1,0:T(8,128)S(1)} %pad_maximum_fusion) | data formatting | bytes 2985984 | tf_op jit(solution)/shard_map/reshape | solution.py:278
  114.2 35.7 %exchange_column.1 = f32[4,729,128]{2,1,0:T(8,128)} custom-call(f32[4,729,128]{2,1,0:T(8,128)} %reshape.78.refs_0_), custom_call_target="tpu_custom_call" | custom-call | tf_op jit(solution)/shard_map/exchange_column/pallas_call | solution.py:118
  149.8 1.5 reduce_sum.9
  151.3 0.5 reshape_reshape.3
  151.8 1.8 convolution_bitcast_fusion.1
  153.6 3.3 %copy.15 = f32[288,18,36]{2,1,0:T(8,128)S(1)} copy(f32[288,18,36]{0,2,1:T(8,128)} %convolution_bitcast_fusion.1) | data formatting | bytes 1492992 | tf_op jit(solution)/shard_map/ga,pza->gzp/transpose | solution.py:23
  156.9 1.8 reshape.79
  158.7 1.2 pad.9
  159.8 0.1 broadcast_in_dim.7
  160.0 1.3 broadcast_in_dim.8
  161.3 39.2 %exchange_all.1 = f32[32,92,128]{2,1,0:T(8,128)} custom-call(f32[32,92,128]{2,1,0:T(8,128)} %bitcast.41), custom_call_target="tpu_custom_call" | custom-call | tf_op jit(solution)/shard_map/exchange_all/pallas_call | solution.py:118
  200.5 2.3 copy.22
  202.8 5.1 %reshape.82 = f32[4,8,18,18,36]{4,3,2,1,0:T(8,128)} reshape(f32[32,11664]{1,0:T(8,128)S(1)} %bitcast.43) | data formatting | bytes 2985984 | tf_op jit(solution)/shard_map/reshape | solution.py:294
  207.9 8.8 %copy.16 = f32[18,8,18,4,36]{4,3,2,1,0:T(4,128)} copy(f32[18,8,18,4,36]{4,2,0,1,3:T(8,128)} %bitcast.37) | data formatting | bytes 2985984 | tf_op jit(solution)/shard_map/transpose | solution.py:298
  216.7 4.5 %reshape.83 = f32[18,144,144]{2,1,0:T(8,128)S(1)} reshape(f32[18,8,18,4,36]{4,3,2,1,0:T(4,128)} %copy.16) | data formatting | bytes 2985984 | tf_op jit(solution)/shard_map/reshape | solution.py:298
  221.2 0.0 copy-start.2
  221.2 3.1 %fusion.9 = f32[144,18,144]{2,0,1:T(8,128)S(1)} fusion(f32[18,144,144]{2,1,0:T(8,128)S(1)} %reshape.83, f32[288,144]{0,1:T(8,128)S(1)} %copy-done.3, s32[]{:T(128)S(6)} %select_n.42), kind=kOutput, calls=%fused_computation.14 | convolution fusion | flops 322486272 | bytes 4294660 | tf_op jit(solution)/shard_map/gzb,fb->gfz/dot_general | solution.py:23
  224.4 4.2 %fusion = f32[18,144,288]{2,1,0:T(8,128)} fusion(f32[288,144,1]{0,1,2:T(8,128)S(1)} %copy-done.2, f32[144,18,144]{2,0,1:T(8,128)S(1)} %fusion.9), kind=kOutput, calls=%fused_computation.2 | convolution fusion | flops 644972544 | bytes 4644864 | tf_op jit(solution)/shard_map/gfz,hz->gfh/dot_general | solution.py:23
  (7 shorter events, 0.0 us)
Async XLA Ops:
  107.2 3.1 %copy-start = (f32[144,24,160]{2,1,0:T(8,128)S(1)}, f32[144,24,160]{2,1,0:T(8,128)}, u32[]{:S(2)}) copy-start(f32[144,24,160]{2,1,0:T(8,128)} %planes.1) | copy-start | bytes 6635524
  114.2 37.6 %copy-start.1 = (f32[288,144,1]{0,1,2:T(8,128)S(1)}, f32[288,144,1]{0,1,2:T(8,128)}, u32[]{:S(2)}) copy-start(f32[288,144,1]{0,1,2:T(8,128)} %constant.86) | copy-start | bytes 497668
  216.7 4.5 %copy-start.3 = (f32[288,144]{0,1:T(8,128)S(1)}, f32[288,144]{0,1:T(8,128)}, u32[]{:S(2)}) copy-start(f32[288,144]{0,1:T(8,128)} %constant.78.clone) | copy-start | bytes 497668
  221.2 3.2 %copy-start.2 = (f32[288,144,1]{0,1,2:T(8,128)S(1)}, f32[288,144,1]{0,1,2:T(8,128)}, u32[]{:S(2)}) copy-start(f32[288,144,1]{0,1,2:T(8,128)} %constant.87) | copy-start | bytes 497668

commit v4 on v3

--- a/solution.py
+++ b/solution.py
@@ -13,7 +13,7 @@
 KZ = 72
 NCOLS = KZ * KZ
 LANES = 128
-LAYERS = 4
+LAYERS = 2
 FOLD_WAVES = 40
 FOLD_POINTS = 80
 MESH = pl.DeviceIdType.MESH
@@ -295,8 +295,11 @@
 
     col_share = NF // fft_size
     own = lax.dynamic_slice_in_dim(interpolation, lax.axis_index("fft") * col_share, col_share, 0)
-    wide = wide.transpose(2, 1, 3, 0, 4).reshape(row_share, group * planes, NC)
-    full = product("gzb,fb->gfz", wide, own)
+    full = 0.0
+    for half in range(LAYERS):
+        own_half = own[:, half * points : (half + 1) * points]
+        full = full + product("tgzb,fb->gftz", wide[half], own_half)
+    full = full.reshape(row_share, col_share, group * planes)
     last = jnp.asarray(np.pad(interpolation_matrix(), ((0, 0), (0, group * planes - NC))))
     return product("gfz,hz->gfh", full, last)
 

time: 229 us -> 204 us (0.89)
  local copies, waits for them, and re-layouts: 43.9 us -> 26.1 us
  Pallas kernels: 167 us -> 157 us
  matrix products: 12.1 us -> 16.2 us
    reshape x2 -> x0, local copies, waits for them, and re-layouts: 9.59 us -> none  [the longest x1 5.08 us: local(): wide.reshape(total, -1)[:, :chunk]]
    pallas_call x3, Pallas kernels: 112 us -> 104 us  [exchange(): pl.pallas_call(lambda *refs: exchange_kernel(scope, *refs), out_shape=jax...]
    transpose x1 -> x0, local copies, waits for them, and re-layouts: 8.76 us -> none  [local(): wide = wide.transpose(2, 1, 3, 0, 4).reshape(row_share, group * planes, NC)]
    squeeze x0 -> x2, local copies, waits for them, and re-layouts: none -> 5.69 us  [local(): full = full + product('tgzb,fb->gftz', wide[half], own_half)]
    dot_general x4 -> x5, matrix products: 12.1 us -> 16.2 us  [product(): jnp.einsum(pattern, operand_a, operand_b, precision=lax.Precision.HIGH)]
    slice x1, local copies, waits for them, and re-layouts: 2.67 us -> 0.37 us  [local(): density[..., FOLD_POINTS + 1:FOLD_POINTS + 1 + NC - kept]]
where the time goes in v4:
time: 204 us
  Pallas kernels  157 us (77%)
  local copies, waits for them, and re-layouts  26.1 us (13%)
  matrix products  16.2 us (8%)
  other arithmetic  3.5 us (2%)
    pallas_call x3, Pallas kernels, exchange(): pl.pallas_call(lambda *refs: exchange_kernel(scope, *refs), out_shape=jax...  104 us
    pallas_call x1, Pallas kernels, local(): pl.pallas_call(lambda *refs: plane_kernel(cols, *refs), out_shape=jax.Sha...  53.6 us
    dot_general x5, matrix products, product(): jnp.einsum(pattern, operand_a, operand_b, precision=lax.Precision.HIGH)  16.2 us
    squeeze x2, local copies, waits for them, and re-layouts, local(): full = full + product('tgzb,fb->gftz', wide[half], own_half)  5.69 us
    transpose x2, local copies, waits for them, and re-layouts, product(): jnp.einsum(pattern, operand_a, operand_b, precision=lax.Precision.HIGH)  4.69 us

profile of v4, /device:TPU:15, one launch (start us, length us, event | category | flops | bytes accessed | tf_op | source)
XLA Modules:
  0.0 203.7 jit_solution(14588266737492012907)
XLA Ops:
  0.0 0.8 fusion.15
  0.8 0.1 fusion.10
  1.7 3.0 %convolution_bitcast_fusion = f32[144,1,2,2592]{3,0,2,1:T(8,128)S(1)} fusion(f32[144,2,2,72]{3,0,2,1:T(8,128)} %constant.75.clone, f32[1,2,72,2592]{3,2,1,0:T(8,128)} %param.8, f32[]{:T(128)} %bitcast.1, f32[72,2592]{1,0:T(8,128)S(1)} %fusion.10), kind=kOutput, calls=%fused_computation | convolution fusion | flops 645719040 | bytes 5391364 | tf_op jit(solution)/shard_map/zpqk,bqkc->zbpc/dot_general | solution.py:23
  4.7 3.2 %copy.14 = f32[144,1,2,2592]{3,2,0,1:T(2,128)} copy(f32[144,1,2,2592]{3,0,2,1:T(8,128)S(1)} %convolution_bitcast_fusion) | data formatting | bytes 5971968 | tf_op jit(solution)/shard_map/zpqk,bqkc->zbpc/transpose | solution.py:23
  7.9 47.2 %exchange_layer.1 = f32[16,9,2,2592]{3,2,1,0:T(2,128)} custom-call(f32[16,9,2,2592]{3,2,1,0:T(2,128)} %bitcast.37), custom_call_target="tpu_custom_call" | custom-call | tf_op jit(solution)/shard_map/exchange_layer/pallas_call | solution.py:118
  55.1 2.9 %copy.15 = f32[8,2,9,2,2592]{4,3,2,0,1:T(2,128)S(1)} copy(f32[8,2,9,2,2592]{4,3,2,1,0:T(2,128)} %bitcast.38) | data formatting | bytes 5971968 | tf_op jit(solution)/shard_map/reshape | solution.py:237
  58.0 0.2 copy.16
  58.3 2.8 %pad.8.refs_0_ = f32[2,2,128,2688]{3,2,1,0:T(8,128)} pad(f32[2,2,72,2592]{3,2,1,0:T(8,128)S(1)} %copy.16, f32[]{:T(128)} %constant.73.clone.1), padding=0_0x0_0x0_56x0_96 | pad | bytes 8491012 | tf_op jit(solution)/shard_map/jit(_pad)/pad | solution.py:242
  61.0 0.7 select_add_fusion.refs_1_
  61.7 53.6 %planes.1 = f32[144,16,160]{2,1,0:T(8,128)} custom-call(f32[2,2,128,2688]{3,2,1,0:T(8,128)} %pad.8.refs_0_, s32[5184]{0:T(1024)} %select_add_fusion.refs_1_, bf16[2,80,120]{2,1,0:T(8,128)(2,1)} %constant.77.clone.refs_2_, bf16[16,256]{1,0:T(8,128)(2,1)} %constant.76.clone.refs_3_), custom_call_target="tpu_custom_call" | custom-call | tf_op jit(solution)/shard_map/planes/pallas_call | solution.py:252
  115.3 1.5 slice.32
  116.8 0.5 copy-done
  117.3 0.4 slice.33
  117.7 0.7 pad_maximum_fusion
  118.4 1.8 reshape.80.refs_0_
  120.1 14.1 %exchange_column.1 = f32[2,729,128]{2,1,0:T(8,128)} custom-call(f32[2,729,128]{2,1,0:T(8,128)} %reshape.80.refs_0_), custom_call_target="tpu_custom_call" | custom-call | tf_op jit(solution)/shard_map/exchange_column/pallas_call | solution.py:118
  134.2 1.2 reduce_sum.9
  135.4 0.3 reshape_reshape.3
  135.7 0.9 convolution_bitcast_fusion.1
  136.7 1.5 copy.18
  138.1 0.6 reshape.81
  138.8 0.1 pad.9
  138.8 0.1 broadcast_in_dim.7
  138.9 1.3 broadcast_in_dim.8
  140.3 42.2 %exchange_all.1 = f32[32,92,128]{2,1,0:T(8,128)} custom-call(f32[32,92,128]{2,1,0:T(8,128)} %bitcast.41), custom_call_target="tpu_custom_call" | custom-call | tf_op jit(solution)/shard_map/exchange_all/pallas_call | solution.py:118
  182.5 2.3 %copy.39 = f32[4,8,92,128]{3,1,2,0:T(8,128)S(1)} copy(f32[4,8,92,128]{3,2,1,0:T(8,128)} %bitcast.42) | data formatting | bytes 3014656
  184.8 1.0 fusion.20
  185.7 2.3 %squeeze.6 = f32[16,18,9,72]{3,2,1,0:T(8,128)} reshape(f32[16,11664]{1,0:T(8,128)S(1)} %get-tuple-element.6) | data formatting | bytes 1492992 | tf_op jit(solution)/shard_map/squeeze | solution.py:301
  188.1 3.4 %fusion.3 = f32[144,16,18,9]{0,2,3,1:T(8,128)S(1)} fusion(f32[16,18,9,72]{3,2,1,0:T(8,128)} %squeeze.6, f32[288,144]{0,1:T(8,128)} %constant.78.clone, s32[]{:T(128)S(6)} %select_n.42), kind=kOutput, calls=%fused_computation.6 | convolution fusion | flops 161243136 | bytes 3926020 | tf_op jit(solution)/shard_map/tgzb,fb->gftz/dot_general | solution.py:23
  191.5 3.4 %squeeze.7 = f32[16,18,9,72]{3,2,1,0:T(8,128)} reshape(f32[16,11664]{1,0:T(8,128)} %get-tuple-element.5) | data formatting | bytes 1492992 | tf_op jit(solution)/shard_map/squeeze | solution.py:301
  194.9 3.6 %convolution_add_fusion = f32[144,16,18,9]{0,2,3,1:T(8,128)S(1)} fusion(f32[144,16,18,9]{0,2,3,1:T(8,128)S(1)} %fusion.3, f32[16,18,9,72]{3,2,1,0:T(8,128)} %squeeze.7, f32[288,144]{0,1:T(8,128)} %constant.78.clone, s32[]{:T(128)S(6)} %select_n.42, s32[]{:T(128)S(6)} %add.73), kind=kOutput, calls=%fused_computation.4 | convolution fusion | flops 161616384 | bytes 5419016 | tf_op jit(solution)/shard_map/tgzb,fb->gftz/dot_general | solution.py:23
  198.5 5.2 %fusion = f32[18,144,288]{2,1,0:T(8,128)} fusion(f32[288,144,1]{0,1,2:T(8,128)S(1)} %copy-done.2, f32[18,144,144]{1,0,2:T(8,128)S(1)} %bitcast.40), kind=kOutput, calls=%fused_computation.1 | convolution fusion | flops 644972544 | bytes 4644864 | tf_op jit(solution)/shard_map/gfz,hz->gfh/dot_general | solution.py:23
  (8 shorter events, 0.0 us)
Async XLA Ops:
  58.3 2.8 %copy-start.3 = (s32[5184]{0:T(1024)S(1)}, s32[5184]{0:T(1024)}, u32[]{:S(2)}) copy-start(s32[5184]{0:T(1024)} %param.9) | copy-start | bytes 62212
  115.3 2.0 copy-start
  120.1 15.6 %copy-start.1 = (f32[288,144,1]{0,1,2:T(8,128)S(1)}, f32[288,144,1]{0,1,2:T(8,128)}, u32[]{:S(2)}) copy-start(f32[288,144,1]{0,1,2:T(8,128)} %constant.86) | copy-start | bytes 497668
  194.9 3.6 %copy-start.2 = (f32[288,144,1]{0,1,2:T(8,128)S(1)}, f32[288,144,1]{0,1,2:T(8,128)}, u32[]{:S(2)}) copy-start(f32[288,144,1]{0,1,2:T(8,128)} %constant.87) | copy-start | bytes 497668

commit v5 on v4

--- a/solution.py
+++ b/solution.py
@@ -188,7 +188,7 @@
         half_im[at, :] = imag
         return carry
 
-    lax.fori_loop(0, KZ, second, 0, unroll=4)
+    lax.fori_loop(0, KZ, second, 0, unroll=6)
 
     def third(point, carry):
         slot = jnp.where(point <= NC // 2, point, point + FOLD_POINTS - NC // 2)
@@ -206,7 +206,7 @@
         )
         return carry
 
-    lax.fori_loop(0, NC, third, 0, unroll=4)
+    lax.fori_loop(0, NC, third, 0, unroll=6)
 
 
 def local(coefficients, col_index, occupation):

time: 204 us -> 200 us (0.980)
  Pallas kernels: 157 us -> 153 us
    pallas_call x1, Pallas kernels: 53.6 us -> 49.2 us  [local(): pl.pallas_call(lambda *refs: plane_kernel(cols, *refs), out_shape=jax.Sha...]
where the time goes in v5:
time: 200 us; the launch traced here: 199 us
  Pallas kernels  153 us (76%)
  local copies, waits for them, and re-layouts  26.1 us (13%)
  matrix products  16.2 us (8%)
  other arithmetic  3.5 us (2%)
    pallas_call x3, Pallas kernels, exchange(): pl.pallas_call(lambda *refs: exchange_kernel(scope, *refs), out_shape=jax...  104 us
    pallas_call x1, Pallas kernels, local(): pl.pallas_call(lambda *refs: plane_kernel(cols, *refs), out_shape=jax.Sha...  49.2 us
    dot_general x5, matrix products, product(): jnp.einsum(pattern, operand_a, operand_b, precision=lax.Precision.HIGH)  16.2 us
    squeeze x2, local copies, waits for them, and re-layouts, local(): full = full + product('tgzb,fb->gftz', wide[half], own_half)  5.69 us
    transpose x2, local copies, waits for them, and re-layouts, product(): jnp.einsum(pattern, operand_a, operand_b, precision=lax.Precision.HIGH)  4.69 us

profile of v5, /device:TPU:15, one launch (start us, length us, event | category | flops | bytes accessed | tf_op | source)
XLA Modules:
  0.0 199.3 jit_solution(18147832528256087141)
XLA Ops:
  0.0 0.8 fusion.15
  0.8 0.1 fusion.10
  1.7 3.0 %convolution_bitcast_fusion = f32[144,1,2,2592]{3,0,2,1:T(8,128)S(1)} fusion(f32[144,2,2,72]{3,0,2,1:T(8,128)} %constant.75.clone, f32[1,2,72,2592]{3,2,1,0:T(8,128)} %param.8, f32[]{:T(128)} %bitcast.1, f32[72,2592]{1,0:T(8,128)S(1)} %fusion.10), kind=kOutput, calls=%fused_computation | convolution fusion | flops 645719040 | bytes 5391364 | tf_op jit(solution)/shard_map/zpqk,bqkc->zbpc/dot_general | solution.py:23
  4.7 3.2 %copy.14 = f32[144,1,2,2592]{3,2,0,1:T(2,128)} copy(f32[144,1,2,2592]{3,0,2,1:T(8,128)S(1)} %convolution_bitcast_fusion) | data formatting | bytes 5971968 | tf_op jit(solution)/shard_map/zpqk,bqkc->zbpc/transpose | solution.py:23
  7.9 47.2 %exchange_layer.1 = f32[16,9,2,2592]{3,2,1,0:T(2,128)} custom-call(f32[16,9,2,2592]{3,2,1,0:T(2,128)} %bitcast.37), custom_call_target="tpu_custom_call" | custom-call | tf_op jit(solution)/shard_map/exchange_layer/pallas_call | solution.py:118
  55.1 2.9 %copy.15 = f32[8,2,9,2,2592]{4,3,2,0,1:T(2,128)S(1)} copy(f32[8,2,9,2,2592]{4,3,2,1,0:T(2,128)} %bitcast.38) | data formatting | bytes 5971968 | tf_op jit(solution)/shard_map/reshape | solution.py:237
  58.0 0.2 copy.16
  58.3 2.8 %pad.8.refs_0_ = f32[2,2,128,2688]{3,2,1,0:T(8,128)} pad(f32[2,2,72,2592]{3,2,1,0:T(8,128)S(1)} %copy.16, f32[]{:T(128)} %constant.73.clone.1), padding=0_0x0_0x0_56x0_96 | pad | bytes 8491012 | tf_op jit(solution)/shard_map/jit(_pad)/pad | solution.py:242
  61.0 0.7 select_add_fusion.refs_1_
  61.7 49.2 %planes.1 = f32[144,16,160]{2,1,0:T(8,128)} custom-call(f32[2,2,128,2688]{3,2,1,0:T(8,128)} %pad.8.refs_0_, s32[5184]{0:T(1024)} %select_add_fusion.refs_1_, bf16[2,80,120]{2,1,0:T(8,128)(2,1)} %constant.77.clone.refs_2_, bf16[16,256]{1,0:T(8,128)(2,1)} %constant.76.clone.refs_3_), custom_call_target="tpu_custom_call" | custom-call | tf_op jit(solution)/shard_map/planes/pallas_call | solution.py:252
  110.9 1.5 slice.32
  112.4 0.5 copy-done
  112.9 0.4 slice.33
  113.3 0.7 pad_maximum_fusion
  114.0 1.8 reshape.80.refs_0_
  115.7 13.9 %exchange_column.1 = f32[2,729,128]{2,1,0:T(8,128)} custom-call(f32[2,729,128]{2,1,0:T(8,128)} %reshape.80.refs_0_), custom_call_target="tpu_custom_call" | custom-call | tf_op jit(solution)/shard_map/exchange_column/pallas_call | solution.py:118
  129.7 1.2 reduce_sum.9
  130.9 0.3 reshape_reshape.3
  131.2 0.9 convolution_bitcast_fusion.1
  132.1 1.5 copy.18
  133.5 0.6 reshape.81
  134.2 0.1 pad.9
  134.2 0.1 broadcast_in_dim.7
  134.4 1.3 broadcast_in_dim.8
  135.7 42.4 %exchange_all.1 = f32[32,92,128]{2,1,0:T(8,128)} custom-call(f32[32,92,128]{2,1,0:T(8,128)} %bitcast.41), custom_call_target="tpu_custom_call" | custom-call | tf_op jit(solution)/shard_map/exchange_all/pallas_call | solution.py:118
  178.1 2.3 %copy.39 = f32[4,8,92,128]{3,1,2,0:T(8,128)S(1)} copy(f32[4,8,92,128]{3,2,1,0:T(8,128)} %bitcast.42) | data formatting | bytes 3014656
  180.4 1.0 fusion.20
  181.3 2.3 %squeeze.6 = f32[16,18,9,72]{3,2,1,0:T(8,128)} reshape(f32[16,11664]{1,0:T(8,128)S(1)} %get-tuple-element.6) | data formatting | bytes 1492992 | tf_op jit(solution)/shard_map/squeeze | solution.py:301
  183.6 3.4 %fusion.3 = f32[144,16,18,9]{0,2,3,1:T(8,128)S(1)} fusion(f32[16,18,9,72]{3,2,1,0:T(8,128)} %squeeze.6, f32[288,144]{0,1:T(8,128)} %constant.78.clone, s32[]{:T(128)S(6)} %select_n.42), kind=kOutput, calls=%fused_computation.6 | convolution fusion | flops 161243136 | bytes 3926020 | tf_op jit(solution)/shard_map/tgzb,fb->gftz/dot_general | solution.py:23
  187.1 3.4 %squeeze.7 = f32[16,18,9,72]{3,2,1,0:T(8,128)} reshape(f32[16,11664]{1,0:T(8,128)} %get-tuple-element.5) | data formatting | bytes 1492992 | tf_op jit(solution)/shard_map/squeeze | solution.py:301
  190.5 3.6 %convolution_add_fusion = f32[144,16,18,9]{0,2,3,1:T(8,128)S(1)} fusion(f32[144,16,18,9]{0,2,3,1:T(8,128)S(1)} %fusion.3, f32[16,18,9,72]{3,2,1,0:T(8,128)} %squeeze.7, f32[288,144]{0,1:T(8,128)} %constant.78.clone, s32[]{:T(128)S(6)} %select_n.42, s32[]{:T(128)S(6)} %add.73), kind=kOutput, calls=%fused_computation.4 | convolution fusion | flops 161616384 | bytes 5419016 | tf_op jit(solution)/shard_map/tgzb,fb->gftz/dot_general | solution.py:23
  194.1 5.2 %fusion = f32[18,144,288]{2,1,0:T(8,128)} fusion(f32[288,144,1]{0,1,2:T(8,128)S(1)} %copy-done.2, f32[18,144,144]{1,0,2:T(8,128)S(1)} %bitcast.40), kind=kOutput, calls=%fused_computation.1 | convolution fusion | flops 644972544 | bytes 4644864 | tf_op jit(solution)/shard_map/gfz,hz->gfh/dot_general | solution.py:23
  (8 shorter events, 0.0 us)
Async XLA Ops:
  58.3 2.8 %copy-start.3 = (s32[5184]{0:T(1024)S(1)}, s32[5184]{0:T(1024)}, u32[]{:S(2)}) copy-start(s32[5184]{0:T(1024)} %param.9) | copy-start | bytes 62212
  110.9 2.0 %copy-start = (f32[144,16,160]{2,1,0:T(8,128)S(1)}, f32[144,16,160]{2,1,0:T(8,128)}, u32[]{:S(2)}) copy-start(f32[144,16,160]{2,1,0:T(8,128)} %planes.1) | copy-start | bytes 4423684
  115.7 15.4 %copy-start.1 = (f32[288,144,1]{0,1,2:T(8,128)S(1)}, f32[288,144,1]{0,1,2:T(8,128)}, u32[]{:S(2)}) copy-start(f32[288,144,1]{0,1,2:T(8,128)} %constant.86) | copy-start | bytes 497668
  190.5 3.6 %copy-start.2 = (f32[288,144,1]{0,1,2:T(8,128)S(1)}, f32[288,144,1]{0,1,2:T(8,128)}, u32[]{:S(2)}) copy-start(f32[288,144,1]{0,1,2:T(8,128)} %constant.87) | copy-start | bytes 497668
